TPU v7x, 512 devices: a whole 4x8x8 slice. The times are simulated.
512 devices in a mesh: dp: 64 (over x, y, core), tensor: 8 (over z).
Axes of the slice: x: 4, y: 8, z: 8, core: 2. Of those that a mesh axis runs over, the one named last changes fastest.
Arguments:
- attn_out: bfloat16 [65536, 3072], P('dp', 'tensor'), may hold values from -6 to 6
- cotangent: bfloat16 [65536, 2560], P(('dp', 'tensor')), may hold values from -0.1875 to 0.1875
- residual: bfloat16 [64, 3072, 2560], P('dp', 'tensor'), may hold values from -6 to 6
- local_offsets: int32 [64, 8, 64, 48], P('dp', 'tensor'), may hold values from 0 to 149, as said below
- local_counts: int32 [64, 8, 64], P('dp', 'tensor'), may hold values from 1 to 48, as said below
- kept_offsets: int32 [8, 64, 12], P('tensor'), may hold values from 0 to 149, as said below
- kept_counts: int32 [8, 64], P('tensor'), may hold values from 6 to 12, as said below
- bounds: int32 [65], replicated, may hold values from 0 to 7680, as said below
Outputs:
- new_residual: bfloat16 [64, 3072, 2560], P('dp', 'tensor')
- kept_sums: float32 [8, 64, 12, 128], P('tensor')
Inputs may be any that keep to these rules, and one draw needn't show every extreme that they name: `local_offsets`: for each replica, band and region the 48 entries are different offsets within the region (below bounds[r + 1] - bounds[r]); slots at or past local_counts are ignored but hold such offsets too. `local_counts`: for each band, some region has 48 live slots from every replica. `kept_offsets`: for each band and region the 12 entries are different offsets within the region; slots at or past kept_counts are ignored. `kept_counts`: for each band, some region has 12 live kept slots. bounds[0] = 0, bounds[64] = 7680, rising; each region holds 90 to 150 blocks.
All inputs are finite; a program needn't handle non-finite values.
Results may differ from a plain program's by a relative error of at most 0.001.
Values may be sent and summed in bfloat16 or wider, within the bound.
A program may use at most 64 MiB of HBM per device.

v0:
```python
import jax
import jax.numpy as jnp
from jax import lax
from jax.sharding import PartitionSpec as P


def cut_along(array, dim, devices):
    before, after = (array.shape[:dim], array.shape[dim + 1 :])
    return jnp.moveaxis(array.reshape(*before, devices, -1, *after), dim, 0)


def sent_and_summed(array, axis, dim):
    parts = cut_along(array, dim, lax.axis_size(axis))
    arrived = lax.all_to_all(parts, axis, split_axis=0, concat_axis=0, tiled=True)
    return arrived.sum(axis=0)


def from_everyone(array, axis):
    devices = lax.axis_size(axis)
    return lax.all_to_all(
        jnp.broadcast_to(array[None], (devices, *array.shape)), axis, 0, 0, tiled=True
    )


def joined_along(parts, dim):
    parts = jnp.moveaxis(parts, 0, dim)
    dims = parts.shape
    return parts.reshape(*dims[:dim], dims[dim] * dims[dim + 1], *dims[dim + 2 :])


def gathered_copies(array, axis, dim):
    parts = from_everyone(array, axis)
    return joined_along(parts, dim)


def on_device(
    attn_out, cotangent, residual, local_offsets, local_counts, kept_offsets, kept_counts, bounds
):
    gradient = lax.dot_general(
        attn_out,
        lax.all_gather(cotangent, "tensor", axis=0, tiled=True),
        (((0,), (0,)), ((), ())),
        preferred_element_type=jnp.float32,
    )
    accumulated = residual[0].astype(jnp.float32) + gradient
    blocks = accumulated.reshape(-1, 128)
    regions = local_offsets.shape[2]
    slot_count = local_offsets.shape[3]
    offsets = local_offsets[0, 0]
    counts = local_counts[0, 0]
    live_slots = jnp.arange(slot_count)[None, :] < counts[:, None]
    region_starts = bounds[:regions]
    where_abs = region_starts[:, None] + offsets
    picked = blocks[where_abs] * live_slots[..., None].astype(jnp.float32)
    sent_mask = (
        jnp.zeros((blocks.shape[0],), jnp.float32)
        .at[where_abs.reshape(-1)]
        .max(live_slots.reshape(-1).astype(jnp.float32))
    )
    new_residual = (
        (blocks * (1.0 - sent_mask[:, None])).reshape(accumulated.shape).astype(jnp.bfloat16)[None]
    )
    kept_here = kept_offsets[0]
    kept_live = jnp.arange(kept_here.shape[1])[None, :] < kept_counts[0][:, None]
    matches = ((kept_here[:, :, None] == offsets[:, None, :]) & kept_live[:, :, None]).astype(
        jnp.float32
    )
    contributions = jnp.einsum("rji,ric->rjc", matches, picked, precision=lax.Precision.HIGHEST)
    owned = sent_and_summed(contributions, "dp", 0)
    summed = gathered_copies(owned, "dp", 0)
    return (new_residual, summed[None])


def solution(mesh):
    in_specs = (
        P("dp", "tensor"),
        P(("dp", "tensor"), None),
        P("dp", "tensor", None),
        P("dp", "tensor", None, None),
        P("dp", "tensor", None),
        P("tensor", None, None),
        P("tensor", None),
        P(),
    )
    out_specs = (P("dp", "tensor", None), P("tensor", None, None, None))
    return jax.shard_map(
        on_device, mesh=mesh, in_specs=in_specs, out_specs=out_specs, check_vma=False
    )
```

profile of v0, /device:TPU:1, one launch (start us, length us, event | category | flops | bytes accessed | tf_op | source)
XLA Modules:
  0.0 182.2 jit_solution(15922232278247330665)
XLA Ops:
  7.2 0.0 all-gather.2.cloned.1.call-start
  7.2 0.7 all-gather.2.cloned.1.call-update
  7.9 0.7 add.59
  8.6 0.1 add.60
  8.7 0.8 copy.26
  9.6 0.1 squeeze.6
  9.7 0.7 fusion.12
  10.4 0.1 reshape.166
  10.5 0.8 compare_select_fusion.1
  11.2 0.1 copy.31
  11.3 0.1 reshape.156
  11.4 0.8 copy.30
  12.2 0.8 copy.34
  13.0 0.7 iota_compare_fusion
  13.7 69.7 %all-gather.2.cloned.1.call-done = bf16[1024,2560]{1,0:T(8,128)(2,1)} async-done(((bf16[128,2560]{1,0:T(8,128)(2,1)}), bf16[1024,2560]{1,0:T(8,128)(2,1)}) %all-gather.2.cloned.1.call-update) | async-done | bytes 5242896 | tf_op jit(solution)/shard_map/all_gather | solution.py:41
  83.4 7.2 %convolution_add_fusion = f32[384,2560]{1,0:T(8,128)} fusion(bf16[1024,384]{1,0:T(8,128)(2,1)S(1)} %copy-done, bf16[1024,2560]{1,0:T(8,128)(2,1)} %all-gather.2.cloned.1.call-done, bf16[1,384,2560]{2,1,0:T(8,128)(2,1)} %param.10), kind=kOutput, calls=%fused_computation.2 | convolution fusion | flops 2015232000 | bytes 11927552 | tf_op jit(solution)/shard_map/dot_general | solution.py:39
  90.6 4.7 %reshape.150 = f32[7680,128]{1,0:T(8,128)} reshape(f32[384,2560]{1,0:T(8,128)} %convolution_add_fusion) | data formatting | bytes 7864320 | tf_op jit(solution)/shard_map/reshape | solution.py:46
  95.3 10.2 %gather_fusion = f32[3072,128]{1,0:T(8,128)S(1)} fusion(f32[7680,128]{1,0:T(8,128)} %reshape.150, s32[3072]{0:T(1024)S(1)} %broadcast_clamp_fusion), kind=kCustom, calls=%fused_computation | custom fusion | bytes 3158016 | tf_op jit(solution)/shard_map/gather | solution.py:54
  105.6 1.9 %fusion.3 = f32[64,1,12,128]{3,2,0,1:T(8,128)S(1)} fusion(f32[64,48,128]{2,1,0:T(8,128)S(1)} %bitcast.27, f32[64,48]{1,0:T(8,128)S(1)} %fusion.12, s32[64,48]{1,0:T(8,128)S(1)} %copy.30, s32[64,12]{1,0:T(8,128)S(1)} %bitcast.30, pred[64,12]{1,0:T(8,128)(4,1)S(1)} %iota_compare_fusion), kind=kOutput, calls=%fused_computation.7 | convolution fusion | flops 57090048 | bytes 1994496 | tf_op jit(solution)/shard_map/rji,ric->rjc/dot_general | solution.py:68
  107.4 1.2 copy.32
  108.6 10.5 %all-to-all-start = ((f32[64,1,12,128]{3,1,2,0:T(1,128)}), f32[64,1,12,128]{3,1,2,0:T(1,128)S(1)}, u32[]{:S(2)}, u32[]{:S(2)}) async-start(f32[64,1,12,128]{3,1,2,0:T(1,128)} %copy.32), calls=%async_computation | async-start | bytes 786432 | tf_op jit(solution)/shard_map/all_to_all | solution.py:14
  119.2 21.3 %scatter_custom_fusion = f32[7680]{0:T(1024)S(1)} fusion(s32[3072]{0:T(1024)S(1)} %bitcast.31, f32[3072]{0:T(1024)S(1)} %reshape.166, f32[]{:T(128)} %constant.5.clone.1), kind=kCustom, calls=%fused_computation.20 | custom fusion | flops 3072 | bytes 30724 | tf_op jit(solution)/shard_map/scatter-max | solution.py:58
  140.5 0.2 mul.21
  140.7 0.1 copy.27
  140.8 2.3 %mul.22 = f32[384,20,128]{0,2,1:T(8,128)} broadcast(f32[384,20]{0,1:T(8,128)S(1)} %copy.27), dimensions={0,1} | broadcast | bytes 3962880 | tf_op jit(solution)/shard_map/mul | solution.py:61
  143.1 5.4 %copy.28 = f32[384,2560]{1,0:T(8,128)} copy(f32[384,2560]{0,1:T(8,128)} %bitcast.26) | data formatting | bytes 7864320 | tf_op jit(solution)/shard_map/mul | solution.py:61
  148.5 0.2 reduce_sum.9
  148.8 0.9 broadcast_in_dim.8
  149.7 10.3 %all-to-all-start.1 = ((f32[64,1,12,128]{3,1,2,0:T(1,128)}), f32[64,1,12,128]{3,1,2,0:T(1,128)S(1)}, u32[]{:S(2)}, u32[]{:S(2)}) async-start(f32[64,1,12,128]{3,1,2,0:T(1,128)} %broadcast_in_dim.8), calls=%async_computation.1 | async-start | bytes 786432 | tf_op jit(solution)/shard_map/all_to_all | solution.py:20
  160.0 5.1 %fusion = bf16[1,384,2560]{2,1,0:T(8,128)(2,1)} fusion(f32[384,2560]{1,0:T(8,128)} %convolution_add_fusion, f32[384,2560]{1,0:T(8,128)} %copy.28), kind=kLoop, calls=%fused_computation.4 | loop fusion | flops 1966080 | bytes 9830400 | tf_op jit(solution)/shard_map/broadcast_in_dim | solution.py:61
  165.1 9.5 %all-to-all-done.1 = f32[64,1,12,128]{3,1,2,0:T(1,128)S(1)} async-done(((f32[64,1,12,128]{3,1,2,0:T(1,128)}), f32[64,1,12,128]{3,1,2,0:T(1,128)S(1)}, u32[]{:S(2)}, u32[]{:S(2)}) %all-to-all-start.1) | async-done | bytes 393248 | tf_op jit(solution)/shard_map/all_to_all | solution.py:20
  174.6 0.8 copy.33
  (6 shorter events, 0.0 us)
Async XLA Ops:
  7.2 76.3 %copy-start = (bf16[1024,384]{1,0:T(8,128)(2,1)S(1)}, bf16[1024,384]{1,0:T(8,128)(2,1)}, u32[]{:S(2)}) copy-start(bf16[1024,384]{1,0:T(8,128)(2,1)} %param.8) | copy-start | bytes 2359300
  7.2 76.2 %all-gather.2.cloned.1.call-start = ((), (), s32[]{:S(2)}) async-start(), calls=%async_computation.2 | async-start | bytes 5898240 | tf_op jit(solution)/shard_map/all_gather | solution.py:41
  108.6 39.9 %all-to-all-start = ((f32[64,1,12,128]{3,1,2,0:T(1,128)}), f32[64,1,12,128]{3,1,2,0:T(1,128)S(1)}, u32[]{:S(2)}, u32[]{:S(2)}) async-start(f32[64,1,12,128]{3,1,2,0:T(1,128)} %copy.32), calls=%async_computation | async-start | bytes 786432 | tf_op jit(solution)/shard_map/all_to_all | solution.py:14
  149.7 24.9 %all-to-all-start.1 = ((f32[64,1,12,128]{3,1,2,0:T(1,128)}), f32[64,1,12,128]{3,1,2,0:T(1,128)S(1)}, u32[]{:S(2)}, u32[]{:S(2)}) async-start(f32[64,1,12,128]{3,1,2,0:T(1,128)} %broadcast_in_dim.8), calls=%async_computation.1 | async-start | bytes 786432 | tf_op jit(solution)/shard_map/all_to_all | solution.py:20
Sparse Core Ops, SparseCore 0:
  10.1 73.3 all-gather.1
where the time goes:
time: 183 us; the launch traced here: 182 us
  waiting for transfers between devices  79.9 us (44%)
  local copies, waits for them, and re-layouts  29.4 us (16%)
  other arithmetic  28.9 us (16%)
  starting transfers between devices  20.9 us (11%)
  between operations  14.1 us (8%)
  matrix products  9.07 us (5%)
    all_gather x1, waiting for transfers between devices, on_device(): lax.all_gather(cotangent, 'tensor', axis=0, tiled=True)  69.7 us
    another operation x1, other arithmetic, on_device(): sent_mask = jnp.zeros((blocks.shape[0],), jnp.float32).at[where_abs.resha...  21.3 us
    all_to_all x1, starting transfers between devices, sent_and_summed(): lax.all_to_all(parts, axis, split_axis=0, concat_axis=0, tiled=True)  10.5 us
    all_to_all x1, starting transfers between devices, from_everyone(): lax.all_to_all(jnp.broadcast_to(array[None], (devices, *array.shape)), ax...  10.3 us
    gather x1, local copies, waits for them, and re-layouts, on_device(): picked = blocks[where_abs] * live_slots[..., None].astype(jnp.float32)  10.2 us
    all_to_all x1, waiting for transfers between devices, from_everyone(): lax.all_to_all(jnp.broadcast_to(array[None], (devices, *array.shape)), ax...  9.49 us
    mul x4, local copies, waits for them, and re-layouts, on_device(): blocks * (1.0 - sent_mask[:, None])  8.02 us
    dot_general x1, matrix products, on_device(): lax.dot_general(attn_out, lax.all_gather(cotangent, 'tensor', axis=0, til...  7.21 us
  transfers between devices with their start and end apart: 3, of which 2 were waited for; matrix products, arithmetic and copies ran while one was open for 22% of the time, Pallas kernels for 0%

commit v1 on v0

v1 whole, which is shorter than its diff:
```python
import functools

import jax
import jax.numpy as jnp
from jax import lax
from jax.experimental import pallas as pl
from jax.experimental.pallas import tpu as pltpu
from jax.sharding import PartitionSpec as P

MESH = pl.DeviceIdType.MESH
BLK = 128
CHUNK = 512
KEPT = 12
F32 = jnp.float32
BF16 = jnp.bfloat16


def kernel(
    cfg,
    attn_hbm, cot_hbm, res_hbm, lo_ref, lc_ref, ko_ref, kc_ref, bounds_ref,
    new_hbm, kept_ref,
    attn_v, own_v, res_v, new_v, at_own, at_pair, at_far, pair, far, acc,
    rho, kappa, hit, idx_v, idx_s,
    contrib, partner_in, share, gathered, totals,
    load_sem, idx_sem, store_sem, ring_send, ring_recv,
    pair_send, pair_recv, rs_send, rs_extra, rs_recv, ag_send, ag_recv, swap_send, swap_recv,
):
    chips, n_z = cfg["chips"], cfg["n_z"]
    half = chips // 2
    n_pair = n_z // 2 - 1
    rows = attn_hbm.shape[1]
    width = cot_hbm.shape[1]
    tokens = cot_hbm.shape[0]
    quarters = width // CHUNK
    per_chunk = CHUNK // BLK
    n_cols = width // BLK
    regions = 2 * chips
    magic = -(-(1 << 20) // n_cols)
    tiles = regions * KEPT // 8
    own_tiles = tiles // chips
    half_tiles = tiles // 2

    dp = lax.axis_index("dp")
    z = lax.axis_index("tensor")
    chip = dp // 2
    core = lax.rem(dp, 2)
    right = lax.rem(z + 1, n_z)
    left = lax.rem(z + n_z - 1, n_z)
    partner = dp + 1 - 2 * core
    lane_row = lax.rem(chip, half)
    owner = chip // half == core

    loads = [
        pltpu.make_async_copy(attn_hbm, attn_v, load_sem.at[0]),
    ]
    for q in range(quarters):
        cols = pl.ds(q * CHUNK, CHUNK)
        loads.append(pltpu.make_async_copy(cot_hbm.at[:, cols], own_v.at[q], load_sem.at[1 + q]))
        loads.append(
            pltpu.make_async_copy(res_hbm.at[:, cols], res_v.at[q], load_sem.at[1 + quarters + q])
        )
    for copy in loads:
        copy.start()

    barrier = pltpu.get_barrier_semaphore()
    for to in (left, right):
        pl.semaphore_signal(
            barrier, inc=1, device_id={"dp": dp, "tensor": to}, device_id_type=MESH
        )
    pl.semaphore_signal(
        barrier, inc=1, device_id={"dp": partner, "tensor": z}, device_id_type=MESH
    )

    def greet(j, carry):
        peer = lax.rem(chip + j, chips)
        pl.semaphore_signal(
            barrier, inc=1, device_id={"dp": 2 * peer + core, "tensor": z}, device_id_type=MESH
        )
        return carry

    lax.fori_loop(1, chips, greet, 0)
    pl.semaphore_wait(barrier, chips + 2)

    def hop(side, step, q):
        to = right if side == 0 else left
        if step == 1:
            src = cot_hbm.at[:, pl.ds(pl.multiple_of(q * CHUNK, CHUNK), CHUNK)]
        elif step <= n_pair:
            src = pair.at[step - 2, q, pl.ds(side * tokens, tokens)]
        else:
            src = pair.at[
                step - 2, q, pl.ds(side * tokens + side * (tokens // 2), tokens // 2)
            ]
        if step <= n_pair:
            dst = pair.at[step - 1, q, pl.ds(side * tokens, tokens)]
        else:
            dst = far.at[q, pl.ds(side * (tokens // 2), tokens // 2)]
        return pltpu.make_async_remote_copy(
            src_ref=src,
            dst_ref=dst,
            send_sem=ring_send.at[side, step - 1, q],
            recv_sem=ring_recv.at[side, step - 1, q],
            device_id={"dp": dp, "tensor": to},
            device_id_type=MESH,
        )

    def first(q, carry):
        hop(0, 1, q).start()
        hop(1, 1, q).start()
        return carry

    lax.fori_loop(0, quarters, first, 0)

    offsets = lo_ref[...]
    live = lax.broadcasted_iota(jnp.int32, offsets.shape, 0) < lc_ref[...]
    starts = bounds_ref[:, 0:regions]
    where_abs = starts + offsets
    where_row = (where_abs * magic) >> 20
    where_col = where_abs - where_row * n_cols
    rho[...] = jnp.full(rho.shape, -1, jnp.int32)
    kappa[...] = jnp.full(kappa.shape, -1, jnp.int32)
    rho[0:regions, 0 : offsets.shape[0]] = jnp.where(live, where_row, -1).T
    kappa[0:regions, 0 : offsets.shape[0]] = where_col.T
    hit[...] = jnp.zeros(hit.shape, F32)

    sent = jnp.where(live, offsets, -1)
    idx_v[...] = jnp.zeros(idx_v.shape, jnp.int32)
    nowhere = rows * n_cols
    for j in range(KEPT):
        wanted = ko_ref[j]
        same = jnp.where(sent == wanted, 1, 0)
        found = jnp.sum(same, axis=0, keepdims=True) * jnp.where(j < kc_ref[...], 1, 0)
        kept_abs = starts + wanted
        kept_row = (kept_abs * magic) >> 20
        position = (kept_abs - kept_row * n_cols) * rows + kept_row
        idx_v[j : j + 1, 0:regions] = jnp.where(found > 0, position, nowhere)
    acc[nowhere : nowhere + 8, :] = jnp.zeros((8, BLK), F32)

    loads[0].wait()

    def turned(source):
        start = pl.multiple_of(source * tokens, tokens)
        return attn_v[pl.ds(start, tokens), :].astype(F32).T.astype(BF16)

    at_own[...] = turned(z)
    index_copy = pltpu.make_async_copy(idx_v, idx_s, idx_sem)
    index_copy.start()

    def accumulate(q, lhs, rhs_ref, start):
        for part in range(CHUNK // 256):
            got = jnp.dot(
                lhs, rhs_ref[:, part * 256 : part * 256 + 256], preferred_element_type=F32
            )
            for b in range(2):
                place = pl.ds(
                    pl.multiple_of((q * per_chunk + part * 2 + b) * rows, rows), rows
                )
                block = got[:, b * BLK : b * BLK + BLK]
                if start is None:
                    acc[place, :] = acc[place, :] + block
                else:
                    col = (part * 2 + b) * BLK
                    acc[place, :] = start[:, col : col + BLK].astype(F32) + block

    for copy in loads[1:]:
        copy.wait()

    def own_step(q, carry):
        accumulate(q, at_own[...], own_v.at[q], res_v.at[q])
        return carry

    lax.fori_loop(0, quarters, own_step, 0)
    for d in range(1, n_pair + 1):
        at_pair[d - 1, :, 0:tokens] = turned(lax.rem(z + n_z - d, n_z))
        at_pair[d - 1, :, tokens : 2 * tokens] = turned(lax.rem(z + d, n_z))
    at_far[...] = turned(lax.rem(z + n_z // 2, n_z))

    mask_loops = range(2, n_pair + 1) if n_pair > 1 else range(1, n_pair + 1)
    per_visit = -(-regions // (quarters * len(mask_loops)))
    row_of = lax.broadcasted_iota(jnp.int32, (rows, BLK), 0)
    col_of = lax.broadcasted_iota(jnp.int32, (BLK, BLK), 0)

    def mark(visit):
        total = hit[...]
        for i in range(per_visit):
            r = visit * per_visit + i
            in_row = jnp.where(row_of == rho[pl.ds(r, 1), :], 1.0, 0.0).astype(BF16)
            in_col = jnp.where(col_of == kappa[pl.ds(r, 1), :], 1.0, 0.0).astype(BF16)
            total = total + lax.dot_general(
                in_row, in_col, (((1,), (1,)), ((), ())), preferred_element_type=F32
            )
        hit[...] = total

    for d in range(1, n_pair + 1):

        def pair_step(q, carry, d=d):
            hop(0, d, q).wait_recv()
            hop(0, d + 1, q).start()
            hop(1, d, q).wait_recv()
            hop(1, d + 1, q).start()
            accumulate(q, at_pair[d - 1], pair.at[d - 1, q], None)
            if d in mask_loops:
                mark((d - mask_loops[0]) * quarters + q)
            return carry

        lax.fori_loop(0, quarters, pair_step, 0)

    def far_step(q, carry):
        hop(0, n_pair + 1, q).wait_recv()
        hop(1, n_pair + 1, q).wait_recv()
        accumulate(q, at_far[...], far.at[q], None)
        return carry

    index_copy.wait()
    lax.fori_loop(0, quarters, far_step, 0)

    def pick(tile, carry):
        first = tile * 8
        j = first // regions
        for m in range(8):
            at = idx_s[j, first - j * regions + m]
            at = jnp.minimum(jnp.maximum(at, 0), nowhere)
            contrib[tile, m : m + 1, :] = acc[pl.ds(at, 1), :]
        return carry

    lax.fori_loop(0, tiles, pick, 0)

    mine = core * half_tiles
    theirs = (1 - core) * half_tiles
    to_partner = pltpu.make_async_remote_copy(
        src_ref=contrib.at[pl.ds(theirs, half_tiles)],
        dst_ref=partner_in,
        send_sem=pair_send,
        recv_sem=pair_recv,
        device_id={"dp": partner, "tensor": z},
        device_id_type=MESH,
    )
    to_partner.start()
    to_partner.wait_recv()

    def add_partner(k, carry):
        share[k] = contrib[mine + k] + partner_in[k]
        return carry

    lax.fori_loop(0, half_tiles, add_partner, 0)

    def scatter(j, send_sem):
        slot = lax.rem(lane_row + j, half)
        return pltpu.make_async_remote_copy(
            src_ref=share.at[pl.ds(slot * own_tiles, own_tiles)],
            dst_ref=gathered.at[chip],
            send_sem=send_sem,
            recv_sem=rs_recv,
            device_id={"dp": 2 * (core * half + slot) + core, "tensor": z},
            device_id_type=MESH,
        )

    def scatter_step(j, carry):
        scatter(j, rs_send).start()
        return carry

    @pl.when(jnp.logical_not(owner))
    def _():
        scatter(0, rs_extra).start()

    lax.fori_loop(1, half, scatter_step, 0)

    for c in range(n_cols):
        keep = hit[:, c : c + 1] < 0.5
        value = acc[c * rows : (c + 1) * rows, :]
        new_v[:, c * BLK : (c + 1) * BLK] = jnp.where(keep, value, 0.0).astype(BF16)
    write = pltpu.make_async_copy(new_v, new_hbm, store_sem)
    write.start()

    def hand_out(j):
        return pltpu.make_async_remote_copy(
            src_ref=totals.at[pl.ds(chip * own_tiles, own_tiles)],
            dst_ref=totals.at[pl.ds(chip * own_tiles, own_tiles)],
            send_sem=ag_send,
            recv_sem=ag_recv,
            device_id={"dp": 2 * lax.rem(chip + j, chips) + core, "tensor": z},
            device_id_type=MESH,
        )

    def hand_step(j, carry):
        hand_out(j).start()
        return carry

    def wait_for(ref, count, sem):
        if count == 0:
            return
        part = ref.at[pl.ds(0, count)]
        pltpu.make_async_copy(part, part, sem).wait()

    @pl.when(owner)
    def _():
        gathered[chip] = share[pl.ds(lane_row * own_tiles, own_tiles)]
        wait_for(gathered, chips - 1, rs_recv)
        total = gathered[0]
        for k in range(1, chips):
            total = total + gathered[k]
        totals[pl.ds(chip * own_tiles, own_tiles)] = total
        lax.fori_loop(1, chips, hand_step, 0)
        wait_for(totals, (half - 1) * own_tiles, ag_recv)

    @pl.when(jnp.logical_not(owner))
    def _():
        wait_for(totals, half_tiles, ag_recv)

    swap = pltpu.make_async_remote_copy(
        src_ref=totals.at[pl.ds(mine, half_tiles)],
        dst_ref=totals.at[pl.ds(mine, half_tiles)],
        send_sem=swap_send,
        recv_sem=swap_recv,
        device_id={"dp": partner, "tensor": z},
        device_id_type=MESH,
    )
    swap.start()

    for d in range(1, n_pair + 2):

        def sent_step(q, carry, d=d):
            hop(0, d, q).wait_send()
            hop(1, d, q).wait_send()
            return carry

        lax.fori_loop(0, quarters, sent_step, 0)
    to_partner.wait_send()
    wait_for(share, (half - 1) * own_tiles, rs_send)

    @pl.when(jnp.logical_not(owner))
    def _():
        scatter(0, rs_extra).wait_send()

    @pl.when(owner)
    def _():
        wait_for(totals, (chips - 1) * own_tiles, ag_send)

    write.wait()
    swap.wait()
    kept_ref[...] = totals[...]


def on_device(
    attn_out, cotangent, residual, local_offsets, local_counts, kept_offsets, kept_counts, bounds
):
    n_dp, n_z = lax.axis_size("dp"), lax.axis_size("tensor")
    chips = n_dp // 2
    tokens, width = cotangent.shape
    rows = attn_out.shape[1]
    regions = local_offsets.shape[2]
    n_pair = n_z // 2 - 1
    quarters = width // CHUNK
    n_cols = width // BLK
    padded = -(-regions // 8) * 8 + 8 * quarters
    anywhere = pl.BlockSpec(memory_space=pl.ANY)
    vmem = pl.BlockSpec(memory_space=pltpu.VMEM)
    dma = pltpu.SemaphoreType.DMA
    tiles = regions * KEPT // 8
    new, kept = pl.pallas_call(
        functools.partial(kernel, {"chips": chips, "n_z": n_z}),
        out_shape=(
            jax.ShapeDtypeStruct((rows, width), BF16),
            jax.ShapeDtypeStruct((tiles, 8, BLK), F32),
        ),
        in_specs=[anywhere] * 3 + [vmem] * 5,
        out_specs=(anywhere, vmem),
        scratch_shapes=[
            pltpu.VMEM(attn_out.shape, BF16),
            pltpu.VMEM((quarters, tokens, CHUNK), BF16),
            pltpu.VMEM((quarters, rows, CHUNK), BF16),
            pltpu.VMEM((rows, width), BF16),
            pltpu.VMEM((rows, tokens), BF16),
            pltpu.VMEM((n_pair, rows, 2 * tokens), BF16),
            pltpu.VMEM((rows, tokens), BF16),
            pltpu.VMEM((n_pair, quarters, 2 * tokens, CHUNK), BF16),
            pltpu.VMEM((quarters, tokens, CHUNK), BF16),
            pltpu.VMEM((rows * n_cols + 8, BLK), F32),
            pltpu.VMEM((padded, BLK), jnp.int32),
            pltpu.VMEM((padded, BLK), jnp.int32),
            pltpu.VMEM((rows, BLK), F32),
            pltpu.VMEM((16, BLK), jnp.int32),
            pltpu.SMEM((16, BLK), jnp.int32),
            pltpu.VMEM((tiles, 8, BLK), F32),
            pltpu.VMEM((tiles // 2, 8, BLK), F32),
            pltpu.VMEM((tiles // 2, 8, BLK), F32),
            pltpu.VMEM((chips, tiles // chips, 8, BLK), F32),
            pltpu.VMEM((tiles, 8, BLK), F32),
            dma((1 + 2 * quarters,)),
            dma,
            dma,
            dma((2, n_pair + 1, quarters)),
            dma((2, n_pair + 1, quarters)),
            dma,
            dma,
            dma,
            dma,
            dma,
            dma,
            dma,
            dma,
            dma,
        ],
        compiler_params=pltpu.CompilerParams(collective_id=0, has_side_effects=True),
    )(
        attn_out,
        cotangent,
        residual[0],
        local_offsets[0, 0].T,
        local_counts[0],
        kept_offsets.transpose(2, 0, 1),
        kept_counts,
        bounds[None],
    )
    return new[None], kept.reshape(KEPT, regions, BLK).transpose(1, 0, 2)[None]


def solution(mesh):
    in_specs = (
        P("dp", "tensor"),
        P(("dp", "tensor"), None),
        P("dp", "tensor", None),
        P("dp", "tensor", None, None),
        P("dp", "tensor", None),
        P("tensor", None, None),
        P("tensor", None),
        P(),
    )
    out_specs = (P("dp", "tensor", None), P("tensor", None, None, None))
    return jax.shard_map(
        on_device, mesh=mesh, in_specs=in_specs, out_specs=out_specs, check_vma=False
    )
```

time: 183 us -> 97.3 us (0.53)
  Pallas kernels: 0 us -> 92.7 us
  waiting for transfers between devices: 79.9 us -> 0 us
  other arithmetic: 28.9 us -> 0 us
  local copies, waits for them, and re-layouts: 29.4 us -> 3.74 us
  starting transfers between devices: 20.9 us -> 0 us
  between operations: 14.1 us -> 0.65 us
  matrix products: 9.07 us -> 0 us
    pallas_call x0 -> x1, Pallas kernels: none -> 92.7 us  [on_device(): pl.pallas_call(functools.partial(kernel, {'chips': chips, 'n_z': n_z}), o...]
    all_gather x1 -> x0, waiting for transfers between devices: 69.7 us -> none  [on_device(): lax.all_gather(cotangent, 'tensor', axis=0, tiled=True)]
    another operation x1 -> x0, other arithmetic: 21.3 us -> none  [on_device(): sent_mask = jnp.zeros((blocks.shape[0],), jnp.float32).at[where_abs.resha...]
    all_to_all x2 -> x0, starting transfers between devices: 20.9 us -> none  [the longest x1 10.5 us: sent_and_summed(): lax.all_to_all(parts, axis, split_axis=0, concat_axis=0, tiled=True)]
    gather x1 -> x0, local copies, waits for them, and re-layouts: 10.2 us -> none  [on_device(): picked = blocks[where_abs] * live_slots[..., None].astype(jnp.float32)]
    all_to_all x2 -> x0, waiting for transfers between devices: 9.49 us -> none  [the longest x1 9.49 us: from_everyone(): lax.all_to_all(jnp.broadcast_to(array[None], (devices, *array.shape)), ax...]
    dot_general x2 -> x0, matrix products: 9.07 us -> none  [the longest x1 7.21 us: on_device(): lax.dot_general(attn_out, lax.all_gather(cotangent, 'tensor', axis=0, til...]
    mul x4 -> x0, local copies, waits for them, and re-layouts: 8.02 us -> none  [on_device(): blocks * (1.0 - sent_mask[:, None])]
  transfers between devices with their start and end apart: 3 -> 0, of which waited for: 2 -> 0; matrix products, arithmetic and copies ran while one was open for 22% -> 0% of each run, Pallas kernels for 0% -> 0%
where the time goes in v1:
time: 97.3 us; the launch traced here: 97.1 us
  Pallas kernels  92.7 us (95%)
  local copies, waits for them, and re-layouts  3.74 us (4%)
    pallas_call x1, Pallas kernels, on_device(): pl.pallas_call(functools.partial(kernel, {'chips': chips, 'n_z': n_z}), o...  92.7 us
    unnamed x4, local copies, waits for them, and re-layouts  3.74 us

profile of v1, /device:TPU:1, one launch (start us, length us, event | category | flops | bytes accessed | tf_op | source)
XLA Modules:
  0.0 97.1 jit_solution(12921470037006997751)
XLA Ops:
  0.6 92.7 %shard_map.95 = (bf16[384,2560]{1,0:T(8,128)(2,1)}, f32[96,8,128]{2,1,0:T(8,128)}) custom-call(bf16[1024,384]{1,0:T(8,128)(2,1)} %attn_hbm.1, bf16[128,2560]{1,0:T(8,128)(2,1)} %cot_hbm.1, bf16[384,2560]{1,0:T(8,128)(2,1)} %bitcast.13, s32[48,64]{1,0:T(8,128)} %bitcast.16, s32[1,64]{1,0:T(1,128)} %bitcast.18, s32[12,1,64]{2,1,0:T(1,128)} %bitcast.17, ...), custom_call_target="tpu_custom_call" | custom-call | tf_op jit(solution)/shard_map/pallas_call | solution.py:360
  93.4 0.0 copy-start
  93.4 3.0 %copy.12 = bf16[1,384,2560]{2,1,0:T(8,128)(2,1)} copy(bf16[1,384,2560]{2,1,0:T(8,128)(2,1)} %bitcast.14) | data formatting | bytes 3932160
  96.4 0.0 copy-done
  96.4 0.7 copy.13
Async XLA Ops:
  93.4 3.0 %copy-start = (f32[96,8,128]{2,1,0:T(8,128)S(1)}, f32[96,8,128]{2,1,0:T(8,128)}, u32[]{:S(2)}) copy-start(f32[96,8,128]{2,1,0:T(8,128)} %get-tuple-element.5) | copy-start | bytes 1179652

commit v2 on v1

--- a/solution.py
+++ b/solution.py
@@ -11,6 +11,7 @@
 BLK = 128
 CHUNK = 512
 KEPT = 12
+GRID_Y = 8
 F32 = jnp.float32
 BF16 = jnp.bfloat16
 
@@ -18,12 +19,12 @@
 def kernel(
     cfg,
     attn_hbm, cot_hbm, res_hbm, lo_ref, lc_ref, ko_ref, kc_ref, bounds_ref,
-    new_hbm, kept_ref,
+    new_hbm, kept_hbm,
     attn_v, own_v, res_v, new_v, at_own, at_pair, at_far, pair, far, acc,
     rho, kappa, hit, idx_v, idx_s,
     contrib, partner_in, share, gathered, totals,
     load_sem, idx_sem, store_sem, ring_send, ring_recv,
-    pair_send, pair_recv, rs_send, rs_extra, rs_recv, ag_send, ag_recv, swap_send, swap_recv,
+    word, pair_send, pair_recv, rs_send, rs_extra, rs_recv, ag_send, ag_recv, swap_send, swap_recv,
 ):
     chips, n_z = cfg["chips"], cfg["n_z"]
     half = chips // 2
@@ -49,6 +50,19 @@
     partner = dp + 1 - 2 * core
     lane_row = lax.rem(chip, half)
     owner = chip // half == core
+    n_x, n_y = cfg["n_x"], cfg["n_y"]
+    x, y = chip // n_y, lax.rem(chip, n_y)
+    near_x = [lax.rem(x + step, n_x) * n_y + y for step in sorted({1, n_x - 1}) if n_x > 1]
+    near_y = [x * n_y + lax.rem(y + step, n_y) for step in sorted({1, n_y - 1}) if n_y > 1]
+
+    stages = [near_x] * max(n_x // 2 - 1, 0) + [near_y] * (n_y // 2)
+
+    def pass_word(stage):
+        if 0 < stage <= len(stages):
+            pl.semaphore_wait(word.at[stage - 1], len(stages[stage - 1]))
+        if stage < len(stages):
+            tell(word.at[stage], stages[stage])
+
 
     loads = [
         pltpu.make_async_copy(attn_hbm, attn_v, load_sem.at[0]),
@@ -71,15 +85,14 @@
         barrier, inc=1, device_id={"dp": partner, "tensor": z}, device_id_type=MESH
     )
 
-    def greet(j, carry):
-        peer = lax.rem(chip + j, chips)
-        pl.semaphore_signal(
-            barrier, inc=1, device_id={"dp": 2 * peer + core, "tensor": z}, device_id_type=MESH
-        )
-        return carry
-
-    lax.fori_loop(1, chips, greet, 0)
-    pl.semaphore_wait(barrier, chips + 2)
+    def tell(sem, near):
+        for to in near:
+            pl.semaphore_signal(
+                sem, inc=1, device_id={"dp": 2 * to + core, "tensor": z}, device_id_type=MESH
+            )
+
+    tell(barrier, near_x + near_y)
+    pl.semaphore_wait(barrier, 3 + len(near_x) + len(near_y))
 
     def hop(side, step, q):
         to = right if side == 0 else left
@@ -111,6 +124,8 @@
 
     lax.fori_loop(0, quarters, first, 0)
 
+    pass_word(0)
+
     offsets = lo_ref[...]
     live = lax.broadcasted_iota(jnp.int32, offsets.shape, 0) < lc_ref[...]
     starts = bounds_ref[:, 0:regions]
@@ -135,6 +150,8 @@
         position = (kept_abs - kept_row * n_cols) * rows + kept_row
         idx_v[j : j + 1, 0:regions] = jnp.where(found > 0, position, nowhere)
     acc[nowhere : nowhere + 8, :] = jnp.zeros((8, BLK), F32)
+
+    pass_word(1)
 
     loads[0].wait()
 
@@ -170,6 +187,7 @@
         return carry
 
     lax.fori_loop(0, quarters, own_step, 0)
+    pass_word(2)
     for d in range(1, n_pair + 1):
         at_pair[d - 1, :, 0:tokens] = turned(lax.rem(z + n_z - d, n_z))
         at_pair[d - 1, :, tokens : 2 * tokens] = turned(lax.rem(z + d, n_z))
@@ -203,6 +221,7 @@
                 mark((d - mask_loops[0]) * quarters + q)
             return carry
 
+        pass_word(d + 2)
         lax.fori_loop(0, quarters, pair_step, 0)
 
     def far_step(q, carry):
@@ -211,6 +230,8 @@
         accumulate(q, at_far[...], far.at[q], None)
         return carry
 
+    for stage in range(n_pair + 3, len(stages) + 1):
+        pass_word(stage)
     index_copy.wait()
     lax.fori_loop(0, quarters, far_step, 0)
 
@@ -338,7 +359,31 @@
 
     write.wait()
     swap.wait()
-    kept_ref[...] = totals[...]
+    keep_out = pltpu.make_async_copy(totals, kept_hbm, store_sem)
+    keep_out.start()
+    keep_out.wait()
+
+
+def finish(new_ref, kept_ref, new_out, kept_out, new_v, kept_v, sem_in, sem_out):
+    pieces = new_v.shape[0]
+    each = new_ref.shape[0] // pieces
+    moves = [(kept_ref, kept_v, kept_out)]
+    for i in range(pieces):
+        part = pl.ds(i * each, each)
+        moves.append((new_ref.at[part], new_v.at[i], new_out.at[part]))
+    inward = [
+        pltpu.make_async_copy(a, b, sem_in.at[i]) for i, (a, b, _) in enumerate(moves)
+    ]
+    outward = [
+        pltpu.make_async_copy(b, c, sem_out.at[i]) for i, (_, b, c) in enumerate(moves)
+    ]
+    for copy in inward:
+        copy.start()
+    for got, put in zip(inward, outward):
+        got.wait()
+        put.start()
+    for put in outward:
+        put.wait()
 
 
 def on_device(
@@ -346,6 +391,8 @@
 ):
     n_dp, n_z = lax.axis_size("dp"), lax.axis_size("tensor")
     chips = n_dp // 2
+    n_y = GRID_Y if chips % GRID_Y == 0 else chips
+    n_x = chips // n_y
     tokens, width = cotangent.shape
     rows = attn_out.shape[1]
     regions = local_offsets.shape[2]
@@ -358,13 +405,13 @@
     dma = pltpu.SemaphoreType.DMA
     tiles = regions * KEPT // 8
     new, kept = pl.pallas_call(
-        functools.partial(kernel, {"chips": chips, "n_z": n_z}),
+        functools.partial(kernel, {"chips": chips, "n_z": n_z, "n_x": n_x, "n_y": n_y}),
         out_shape=(
             jax.ShapeDtypeStruct((rows, width), BF16),
             jax.ShapeDtypeStruct((tiles, 8, BLK), F32),
         ),
         in_specs=[anywhere] * 3 + [vmem] * 5,
-        out_specs=(anywhere, vmem),
+        out_specs=(anywhere, anywhere),
         scratch_shapes=[
             pltpu.VMEM(attn_out.shape, BF16),
             pltpu.VMEM((quarters, tokens, CHUNK), BF16),
@@ -391,6 +438,7 @@
             dma,
             dma((2, n_pair + 1, quarters)),
             dma((2, n_pair + 1, quarters)),
+            pltpu.SemaphoreType.REGULAR((n_x + n_y,)),
             dma,
             dma,
             dma,
@@ -412,6 +460,22 @@
         kept_counts,
         bounds[None],
     )
+    pieces = 4
+    new, kept = pl.pallas_call(
+        finish,
+        out_shape=(
+            jax.ShapeDtypeStruct(new.shape, BF16),
+            jax.ShapeDtypeStruct(kept.shape, F32),
+        ),
+        in_specs=[anywhere] * 2,
+        out_specs=(anywhere, anywhere),
+        scratch_shapes=[
+            pltpu.VMEM((pieces, rows // pieces, width), BF16),
+            pltpu.VMEM(kept.shape, F32),
+            dma((pieces + 1,)),
+            dma((pieces + 1,)),
+        ],
+    )(new, kept)
     return new[None], kept.reshape(KEPT, regions, BLK).transpose(1, 0, 2)[None]
 
 

time: 97.3 us -> 93.8 us (0.964)
  local copies, waits for them, and re-layouts: 3.74 us -> 0 us
    unnamed x4 -> x0, local copies, waits for them, and re-layouts: 3.74 us -> none
    pallas_call x1 -> x2, Pallas kernels: 92.7 us -> 93 us  [the longest x1 90.5 us: on_device(): pl.pallas_call(functools.partial(kernel, {'chips': chips, 'n_z': n_z, 'n_...]
where the time goes in v2:
time: 93.8 us; the launch traced here: 93.6 us
  Pallas kernels  93 us (99%)
    pallas_call x1, Pallas kernels, on_device(): pl.pallas_call(functools.partial(kernel, {'chips': chips, 'n_z': n_z, 'n_...  90.5 us
    pallas_call x1, Pallas kernels, on_device(): pl.pallas_call(finish, out_shape=(jax.ShapeDtypeStruct(new.shape, BF16),...  2.5 us

profile of v2, /device:TPU:1, one launch (start us, length us, event | category | flops | bytes accessed | tf_op | source)
XLA Modules:
  0.0 93.6 jit_solution(3424924352429022007)
XLA Ops:
  0.6 90.5 %shard_map.95 = (bf16[384,2560]{1,0:T(8,128)(2,1)}, f32[96,8,128]{2,1,0:T(8,128)}) custom-call(bf16[1024,384]{1,0:T(8,128)(2,1)} %attn_hbm.1, bf16[128,2560]{1,0:T(8,128)(2,1)} %cot_hbm.1, bf16[384,2560]{1,0:T(8,128)(2,1)} %bitcast.13, s32[48,64]{1,0:T(8,128)} %bitcast.14, s32[1,64]{1,0:T(1,128)} %bitcast.16, s32[12,1,64]{2,1,0:T(1,128)} %bitcast.15, ...), custom_call_target="tpu_custom_call" | custom-call | tf_op jit(solution)/shard_map/pallas_call | solution.py:407
  91.1 2.5 %shard_map.96 = (bf16[384,2560]{1,0:T(8,128)(2,1)}, f32[96,8,128]{2,1,0:T(8,128)}) custom-call(bf16[384,2560]{1,0:T(8,128)(2,1)} %get-tuple-element.6.new_ref, f32[96,8,128]{2,1,0:T(8,128)} %get-tuple-element.7.kept_ref), custom_call_target="tpu_custom_call" | custom-call | tf_op jit(solution)/shard_map/pallas_call | solution.py:464

commit v3 on v2

--- a/solution.py
+++ b/solution.py
@@ -18,12 +18,13 @@
 
 def kernel(
     cfg,
-    attn_hbm, cot_hbm, res_hbm, lo_ref, lc_ref, ko_ref, kc_ref, bounds_ref,
+    attn_hbm, cot_hbm, res_hbm, lo_hbm, lc_hbm, ko_hbm, kc_hbm, bounds_hbm,
     new_hbm, kept_hbm,
+    lo_ref, lc_ref, ko_ref, kc_ref, bounds_ref,
     attn_v, own_v, res_v, new_v, at_own, at_pair, at_far, pair, far, acc,
     rho, kappa, hit, idx_v, idx_s,
     contrib, partner_in, share, gathered, totals,
-    load_sem, idx_sem, store_sem, ring_send, ring_recv,
+    small_sem, load_sem, idx_sem, store_sem, ring_send, ring_recv,
     word, pair_send, pair_recv, rs_send, rs_extra, rs_recv, ag_send, ag_recv, swap_send, swap_recv,
 ):
     chips, n_z = cfg["chips"], cfg["n_z"]
@@ -73,7 +74,19 @@
         loads.append(
             pltpu.make_async_copy(res_hbm.at[:, cols], res_v.at[q], load_sem.at[1 + quarters + q])
         )
-    for copy in loads:
+    small = [
+        pltpu.make_async_copy(a, b, small_sem.at[i])
+        for i, (a, b) in enumerate(
+            (
+                (lo_hbm, lo_ref),
+                (lc_hbm, lc_ref),
+                (ko_hbm, ko_ref),
+                (kc_hbm, kc_ref),
+                (bounds_hbm, bounds_ref),
+            )
+        )
+    ]
+    for copy in small + loads:
         copy.start()
 
     barrier = pltpu.get_barrier_semaphore()
@@ -126,6 +139,8 @@
 
     pass_word(0)
 
+    for copy in small:
+        copy.wait()
     offsets = lo_ref[...]
     live = lax.broadcasted_iota(jnp.int32, offsets.shape, 0) < lc_ref[...]
     starts = bounds_ref[:, 0:regions]
@@ -235,19 +250,26 @@
     index_copy.wait()
     lax.fori_loop(0, quarters, far_step, 0)
 
-    def pick(tile, carry):
-        first = tile * 8
-        j = first // regions
-        for m in range(8):
-            at = idx_s[j, first - j * regions + m]
-            at = jnp.minimum(jnp.maximum(at, 0), nowhere)
-            contrib[tile, m : m + 1, :] = acc[pl.ds(at, 1), :]
-        return carry
-
-    lax.fori_loop(0, tiles, pick, 0)
+    def pick_from(base):
+        def pick(piece, carry):
+            got = []
+            for i in range(own_tiles):
+                begin = (base + piece * own_tiles + i) * 8
+                j = begin // regions
+                for m in range(8):
+                    at = idx_s[j, begin - j * regions + m]
+                    at = jnp.minimum(jnp.maximum(at, 0), nowhere)
+                    got.append(acc[pl.ds(at, 1), :])
+            for i in range(own_tiles):
+                for m in range(8):
+                    contrib[base + piece * own_tiles + i, m : m + 1, :] = got[8 * i + m]
+            return carry
+
+        lax.fori_loop(0, half, pick, 0)
 
     mine = core * half_tiles
     theirs = (1 - core) * half_tiles
+    pick_from(theirs)
     to_partner = pltpu.make_async_remote_copy(
         src_ref=contrib.at[pl.ds(theirs, half_tiles)],
         dst_ref=partner_in,
@@ -257,13 +279,9 @@
         device_id_type=MESH,
     )
     to_partner.start()
+    pick_from(mine)
     to_partner.wait_recv()
-
-    def add_partner(k, carry):
-        share[k] = contrib[mine + k] + partner_in[k]
-        return carry
-
-    lax.fori_loop(0, half_tiles, add_partner, 0)
+    share[...] = contrib[pl.ds(mine, half_tiles)] + partner_in[...]
 
     def scatter(j, send_sem):
         slot = lax.rem(lane_row + j, half)
@@ -401,7 +419,7 @@
     n_cols = width // BLK
     padded = -(-regions // 8) * 8 + 8 * quarters
     anywhere = pl.BlockSpec(memory_space=pl.ANY)
-    vmem = pl.BlockSpec(memory_space=pltpu.VMEM)
+    slots = local_offsets.shape[3]
     dma = pltpu.SemaphoreType.DMA
     tiles = regions * KEPT // 8
     new, kept = pl.pallas_call(
@@ -410,9 +428,14 @@
             jax.ShapeDtypeStruct((rows, width), BF16),
             jax.ShapeDtypeStruct((tiles, 8, BLK), F32),
         ),
-        in_specs=[anywhere] * 3 + [vmem] * 5,
+        in_specs=[anywhere] * 8,
         out_specs=(anywhere, anywhere),
         scratch_shapes=[
+            pltpu.VMEM((slots, regions), jnp.int32),
+            pltpu.VMEM((1, regions), jnp.int32),
+            pltpu.VMEM((KEPT, 1, regions), jnp.int32),
+            pltpu.VMEM((1, regions), jnp.int32),
+            pltpu.VMEM((1, regions + 1), jnp.int32),
             pltpu.VMEM(attn_out.shape, BF16),
             pltpu.VMEM((quarters, tokens, CHUNK), BF16),
             pltpu.VMEM((quarters, rows, CHUNK), BF16),
@@ -433,6 +456,7 @@
             pltpu.VMEM((tiles // 2, 8, BLK), F32),
             pltpu.VMEM((chips, tiles // chips, 8, BLK), F32),
             pltpu.VMEM((tiles, 8, BLK), F32),
+            dma((5,)),
             dma((1 + 2 * quarters,)),
             dma,
             dma,

time: 93.8 us -> 91.5 us (0.975)
  Pallas kernels: 93 us -> 90.7 us
    pallas_call x1, Pallas kernels: 90.5 us -> 88.2 us  [on_device(): pl.pallas_call(functools.partial(kernel, {'chips': chips, 'n_z': n_z, 'n_...]
where the time goes in v3:
time: 91.5 us; the launch traced here: 91.3 us
  Pallas kernels  90.7 us (99%)
    pallas_call x1, Pallas kernels, on_device(): pl.pallas_call(functools.partial(kernel, {'chips': chips, 'n_z': n_z, 'n_...  88.2 us
    pallas_call x1, Pallas kernels, on_device(): pl.pallas_call(finish, out_shape=(jax.ShapeDtypeStruct(new.shape, BF16),...  2.5 us

profile of v3, /device:TPU:1, one launch (start us, length us, event | category | flops | bytes accessed | tf_op | source)
XLA Modules:
  0.0 91.3 jit_solution(3803457753039333152)
XLA Ops:
  0.6 88.2 %shard_map.95 = (bf16[384,2560]{1,0:T(8,128)(2,1)}, f32[96,8,128]{2,1,0:T(8,128)}) custom-call(bf16[1024,384]{1,0:T(8,128)(2,1)} %attn_hbm.1, bf16[128,2560]{1,0:T(8,128)(2,1)} %cot_hbm.1, bf16[384,2560]{1,0:T(8,128)(2,1)} %bitcast.13, s32[48,64]{1,0:T(8,128)} %bitcast.14, s32[1,64]{1,0:T(1,128)} %bitcast.16, s32[12,1,64]{2,1,0:T(1,128)} %bitcast.15, ...), custom_call_target="tpu_custom_call" | custom-call | tf_op jit(solution)/shard_map/pallas_call | solution.py:425
  88.8 2.5 %shard_map.96 = (bf16[384,2560]{1,0:T(8,128)(2,1)}, f32[96,8,128]{2,1,0:T(8,128)}) custom-call(bf16[384,2560]{1,0:T(8,128)(2,1)} %get-tuple-element.6.new_ref, f32[96,8,128]{2,1,0:T(8,128)} %get-tuple-element.7.kept_ref), custom_call_target="tpu_custom_call" | custom-call | tf_op jit(solution)/shard_map/pallas_call | solution.py:488

commit v4 on v3

--- a/solution.py
+++ b/solution.py
@@ -25,7 +25,7 @@
     rho, kappa, hit, idx_v, idx_s,
     contrib, partner_in, share, gathered, totals,
     small_sem, load_sem, idx_sem, store_sem, ring_send, ring_recv,
-    word, pair_send, pair_recv, rs_send, rs_extra, rs_recv, ag_send, ag_recv, swap_send, swap_recv,
+    word, pair_send, pair_recv, rs_send, rs_recv, ag_send, ag_recv, swap_send, swap_recv,
 ):
     chips, n_z = cfg["chips"], cfg["n_z"]
     half = chips // 2
@@ -250,59 +250,79 @@
     index_copy.wait()
     lax.fori_loop(0, quarters, far_step, 0)
 
-    def pick_from(base):
-        def pick(piece, carry):
-            got = []
-            for i in range(own_tiles):
-                begin = (base + piece * own_tiles + i) * 8
-                j = begin // regions
-                for m in range(8):
-                    at = idx_s[j, begin - j * regions + m]
-                    at = jnp.minimum(jnp.maximum(at, 0), nowhere)
-                    got.append(acc[pl.ds(at, 1), :])
-            for i in range(own_tiles):
-                for m in range(8):
-                    contrib[base + piece * own_tiles + i, m : m + 1, :] = got[8 * i + m]
-            return carry
-
-        lax.fori_loop(0, half, pick, 0)
+    def far_first(k, n_rows, n_along):
+        step = k // n_rows
+        aside = (step + 1) // 2
+        along = n_along // 2 + aside - 2 * aside * lax.rem(step, 2)
+        return along + n_along * (n_rows - 1 - lax.rem(k, n_rows))
+
+    half_rows = max(half // n_y, 1)
+
+    def slot_of(k):
+        return lax.rem(lane_row + far_first(k, half_rows, half // half_rows), half)
+
+    def pick(base):
+        got = []
+        for i in range(own_tiles):
+            begin = (base + i) * 8
+            j = begin // regions
+            for m in range(8):
+                at = idx_s[j, begin - j * regions + m]
+                at = jnp.minimum(jnp.maximum(at, 0), nowhere)
+                got.append(acc[pl.ds(at, 1), :])
+        for i in range(own_tiles):
+            for m in range(8):
+                contrib[base + i, m : m + 1, :] = got[8 * i + m]
 
     mine = core * half_tiles
     theirs = (1 - core) * half_tiles
-    pick_from(theirs)
-    to_partner = pltpu.make_async_remote_copy(
-        src_ref=contrib.at[pl.ds(theirs, half_tiles)],
-        dst_ref=partner_in,
-        send_sem=pair_send,
-        recv_sem=pair_recv,
-        device_id={"dp": partner, "tensor": z},
-        device_id_type=MESH,
-    )
-    to_partner.start()
-    pick_from(mine)
-    to_partner.wait_recv()
-    share[...] = contrib[pl.ds(mine, half_tiles)] + partner_in[...]
-
-    def scatter(j, send_sem):
-        slot = lax.rem(lane_row + j, half)
+
+    def to_partner(k):
+        at = slot_of(k) * own_tiles
+        return pltpu.make_async_remote_copy(
+            src_ref=contrib.at[pl.ds(theirs + at, own_tiles)],
+            dst_ref=partner_in.at[pl.ds(at, own_tiles)],
+            send_sem=pair_send.at[k],
+            recv_sem=pair_recv.at[k],
+            device_id={"dp": partner, "tensor": z},
+            device_id_type=MESH,
+        )
+
+    def scatter(k):
+        slot = slot_of(k)
         return pltpu.make_async_remote_copy(
             src_ref=share.at[pl.ds(slot * own_tiles, own_tiles)],
             dst_ref=gathered.at[chip],
-            send_sem=send_sem,
+            send_sem=rs_send.at[k],
             recv_sem=rs_recv,
             device_id={"dp": 2 * (core * half + slot) + core, "tensor": z},
             device_id_type=MESH,
         )
 
-    def scatter_step(j, carry):
-        scatter(j, rs_send).start()
-        return carry
+    def partner_step(k, carry):
+        pick(theirs + slot_of(k) * own_tiles)
+        to_partner(k).start()
+        return carry
+
+    def share_piece(k):
+        at = slot_of(k) * own_tiles
+        pick(mine + at)
+        to_partner(k).wait_recv()
+        piece = pl.ds(at, own_tiles)
+        share[piece] = contrib[pl.ds(mine + at, own_tiles)] + partner_in[piece]
+
+    def scatter_step(k, carry):
+        share_piece(k)
+        scatter(k).start()
+        return carry
+
+    lax.fori_loop(0, half, partner_step, 0)
+    lax.fori_loop(0, half - 1, scatter_step, 0)
+    share_piece(half - 1)
 
     @pl.when(jnp.logical_not(owner))
     def _():
-        scatter(0, rs_extra).start()
-
-    lax.fori_loop(1, half, scatter_step, 0)
+        scatter(half - 1).start()
 
     for c in range(n_cols):
         keep = hit[:, c : c + 1] < 0.5
@@ -311,18 +331,18 @@
     write = pltpu.make_async_copy(new_v, new_hbm, store_sem)
     write.start()
 
-    def hand_out(j):
+    def hand_out(k):
         return pltpu.make_async_remote_copy(
             src_ref=totals.at[pl.ds(chip * own_tiles, own_tiles)],
             dst_ref=totals.at[pl.ds(chip * own_tiles, own_tiles)],
             send_sem=ag_send,
             recv_sem=ag_recv,
-            device_id={"dp": 2 * lax.rem(chip + j, chips) + core, "tensor": z},
+            device_id={"dp": 2 * lax.rem(chip + far_first(k, n_x, n_y), chips) + core, "tensor": z},
             device_id_type=MESH,
         )
 
-    def hand_step(j, carry):
-        hand_out(j).start()
+    def hand_step(k, carry):
+        hand_out(k).start()
         return carry
 
     def wait_for(ref, count, sem):
@@ -339,7 +359,7 @@
         for k in range(1, chips):
             total = total + gathered[k]
         totals[pl.ds(chip * own_tiles, own_tiles)] = total
-        lax.fori_loop(1, chips, hand_step, 0)
+        lax.fori_loop(0, chips - 1, hand_step, 0)
         wait_for(totals, (half - 1) * own_tiles, ag_recv)
 
     @pl.when(jnp.logical_not(owner))
@@ -364,12 +384,21 @@
             return carry
 
         lax.fori_loop(0, quarters, sent_step, 0)
-    to_partner.wait_send()
-    wait_for(share, (half - 1) * own_tiles, rs_send)
+
+    def left_step(k, carry):
+        to_partner(k).wait_send()
+        return carry
+
+    def scattered_step(k, carry):
+        scatter(k).wait_send()
+        return carry
+
+    lax.fori_loop(0, half, left_step, 0)
+    lax.fori_loop(0, half - 1, scattered_step, 0)
 
     @pl.when(jnp.logical_not(owner))
     def _():
-        scatter(0, rs_extra).wait_send()
+        scatter(half - 1).wait_send()
 
     @pl.when(owner)
     def _():
@@ -463,10 +492,9 @@
             dma((2, n_pair + 1, quarters)),
             dma((2, n_pair + 1, quarters)),
             pltpu.SemaphoreType.REGULAR((n_x + n_y,)),
-            dma,
-            dma,
-            dma,
-            dma,
+            dma((chips // 2,)),
+            dma((chips // 2,)),
+            dma((chips // 2,)),
             dma,
             dma,
             dma,

time: 91.5 us -> 89.6 us (0.979)
  Pallas kernels: 90.7 us -> 88.8 us
    pallas_call x1, Pallas kernels: 88.2 us -> 86.3 us  [on_device(): pl.pallas_call(functools.partial(kernel, {'chips': chips, 'n_z': n_z, 'n_...]
where the time goes in v4:
time: 89.6 us; the launch traced here: 89.4 us
  Pallas kernels  88.8 us (99%)
    pallas_call x1, Pallas kernels, on_device(): pl.pallas_call(functools.partial(kernel, {'chips': chips, 'n_z': n_z, 'n_...  86.3 us
    pallas_call x1, Pallas kernels, on_device(): pl.pallas_call(finish, out_shape=(jax.ShapeDtypeStruct(new.shape, BF16),...  2.5 us

profile of v4, /device:TPU:1, one launch (start us, length us, event | category | flops | bytes accessed | tf_op | source)
XLA Modules:
  0.0 89.4 jit_solution(14342463068440417527)
XLA Ops:
  0.6 86.3 %shard_map.95 = (bf16[384,2560]{1,0:T(8,128)(2,1)}, f32[96,8,128]{2,1,0:T(8,128)}) custom-call(bf16[1024,384]{1,0:T(8,128)(2,1)} %attn_hbm.1, bf16[128,2560]{1,0:T(8,128)(2,1)} %cot_hbm.1, bf16[384,2560]{1,0:T(8,128)(2,1)} %bitcast.13, s32[48,64]{1,0:T(8,128)} %bitcast.14, s32[1,64]{1,0:T(1,128)} %bitcast.16, s32[12,1,64]{2,1,0:T(1,128)} %bitcast.15, ...), custom_call_target="tpu_custom_call" | custom-call | tf_op jit(solution)/shard_map/pallas_call | solution.py:454
  86.9 2.5 %shard_map.96 = (bf16[384,2560]{1,0:T(8,128)(2,1)}, f32[96,8,128]{2,1,0:T(8,128)}) custom-call(bf16[384,2560]{1,0:T(8,128)(2,1)} %get-tuple-element.6.new_ref, f32[96,8,128]{2,1,0:T(8,128)} %get-tuple-element.7.kept_ref), custom_call_target="tpu_custom_call" | custom-call | tf_op jit(solution)/shard_map/pallas_call | solution.py:516

commit v5 on v4

--- a/solution.py
+++ b/solution.py
@@ -19,12 +19,12 @@
 def kernel(
     cfg,
     attn_hbm, cot_hbm, res_hbm, lo_hbm, lc_hbm, ko_hbm, kc_hbm, bounds_hbm,
-    new_hbm, kept_hbm,
+    new_v, kept_ref,
     lo_ref, lc_ref, ko_ref, kc_ref, bounds_ref,
-    attn_v, own_v, res_v, new_v, at_own, at_pair, at_far, pair, far, acc,
+    attn_v, own_v, res_v, at_own, at_pair, at_far, pair, far, acc,
     rho, kappa, hit, idx_v, idx_s,
     contrib, partner_in, share, gathered, totals,
-    small_sem, load_sem, idx_sem, store_sem, ring_send, ring_recv,
+    small_sem, load_sem, idx_sem, ring_send, ring_recv,
     word, pair_send, pair_recv, rs_send, rs_recv, ag_send, ag_recv, swap_send, swap_recv,
 ):
     chips, n_z = cfg["chips"], cfg["n_z"]
@@ -316,8 +316,14 @@
         scatter(k).start()
         return carry
 
-    lax.fori_loop(0, half, partner_step, 0)
-    lax.fori_loop(0, half - 1, scatter_step, 0)
+    def both_step(k, carry):
+        partner_step(k + ahead, carry)
+        return scatter_step(k, carry)
+
+    ahead = min(6, half)
+    lax.fori_loop(0, ahead, partner_step, 0)
+    lax.fori_loop(0, half - ahead, both_step, 0)
+    lax.fori_loop(half - ahead, half - 1, scatter_step, 0)
     share_piece(half - 1)
 
     @pl.when(jnp.logical_not(owner))
@@ -328,8 +334,6 @@
         keep = hit[:, c : c + 1] < 0.5
         value = acc[c * rows : (c + 1) * rows, :]
         new_v[:, c * BLK : (c + 1) * BLK] = jnp.where(keep, value, 0.0).astype(BF16)
-    write = pltpu.make_async_copy(new_v, new_hbm, store_sem)
-    write.start()
 
     def hand_out(k):
         return pltpu.make_async_remote_copy(
@@ -404,33 +408,19 @@
     def _():
         wait_for(totals, (chips - 1) * own_tiles, ag_send)
 
-    write.wait()
     swap.wait()
-    keep_out = pltpu.make_async_copy(totals, kept_hbm, store_sem)
-    keep_out.start()
-    keep_out.wait()
-
-
-def finish(new_ref, kept_ref, new_out, kept_out, new_v, kept_v, sem_in, sem_out):
-    pieces = new_v.shape[0]
-    each = new_ref.shape[0] // pieces
-    moves = [(kept_ref, kept_v, kept_out)]
-    for i in range(pieces):
-        part = pl.ds(i * each, each)
-        moves.append((new_ref.at[part], new_v.at[i], new_out.at[part]))
-    inward = [
-        pltpu.make_async_copy(a, b, sem_in.at[i]) for i, (a, b, _) in enumerate(moves)
+    kept_ref[...] = totals[...]
+
+
+def finish(new_v, kept_v, new_out, kept_out, sems):
+    copies = [
+        pltpu.make_async_copy(kept_v, kept_out, sems.at[0]),
+        pltpu.make_async_copy(new_v, new_out, sems.at[1]),
     ]
-    outward = [
-        pltpu.make_async_copy(b, c, sem_out.at[i]) for i, (_, b, c) in enumerate(moves)
-    ]
-    for copy in inward:
+    for copy in copies:
         copy.start()
-    for got, put in zip(inward, outward):
-        got.wait()
-        put.start()
-    for put in outward:
-        put.wait()
+    for copy in copies:
+        copy.wait()
 
 
 def on_device(
@@ -448,17 +438,18 @@
     n_cols = width // BLK
     padded = -(-regions // 8) * 8 + 8 * quarters
     anywhere = pl.BlockSpec(memory_space=pl.ANY)
+    vmem = pl.BlockSpec(memory_space=pltpu.VMEM)
     slots = local_offsets.shape[3]
     dma = pltpu.SemaphoreType.DMA
     tiles = regions * KEPT // 8
     new, kept = pl.pallas_call(
         functools.partial(kernel, {"chips": chips, "n_z": n_z, "n_x": n_x, "n_y": n_y}),
         out_shape=(
-            jax.ShapeDtypeStruct((rows, width), BF16),
-            jax.ShapeDtypeStruct((tiles, 8, BLK), F32),
+            pltpu.VMEM((rows, width), BF16),
+            pltpu.VMEM((tiles, 8, BLK), F32),
         ),
         in_specs=[anywhere] * 8,
-        out_specs=(anywhere, anywhere),
+        out_specs=(vmem, vmem),
         scratch_shapes=[
             pltpu.VMEM((slots, regions), jnp.int32),
             pltpu.VMEM((1, regions), jnp.int32),
@@ -468,7 +459,6 @@
             pltpu.VMEM(attn_out.shape, BF16),
             pltpu.VMEM((quarters, tokens, CHUNK), BF16),
             pltpu.VMEM((quarters, rows, CHUNK), BF16),
-            pltpu.VMEM((rows, width), BF16),
             pltpu.VMEM((rows, tokens), BF16),
             pltpu.VMEM((n_pair, rows, 2 * tokens), BF16),
             pltpu.VMEM((rows, tokens), BF16),
@@ -487,7 +477,6 @@
             pltpu.VMEM((tiles, 8, BLK), F32),
             dma((5,)),
             dma((1 + 2 * quarters,)),
-            dma,
             dma,
             dma((2, n_pair + 1, quarters)),
             dma((2, n_pair + 1, quarters)),
@@ -512,21 +501,17 @@
         kept_counts,
         bounds[None],
     )
-    pieces = 4
+    new = pltpu.with_memory_space_constraint(new, pltpu.VMEM)
+    kept = pltpu.with_memory_space_constraint(kept, pltpu.VMEM)
     new, kept = pl.pallas_call(
         finish,
         out_shape=(
             jax.ShapeDtypeStruct(new.shape, BF16),
             jax.ShapeDtypeStruct(kept.shape, F32),
         ),
-        in_specs=[anywhere] * 2,
+        in_specs=[vmem] * 2,
         out_specs=(anywhere, anywhere),
-        scratch_shapes=[
-            pltpu.VMEM((pieces, rows // pieces, width), BF16),
-            pltpu.VMEM(kept.shape, F32),
-            dma((pieces + 1,)),
-            dma((pieces + 1,)),
-        ],
+        scratch_shapes=[dma((2,))],
     )(new, kept)
     return new[None], kept.reshape(KEPT, regions, BLK).transpose(1, 0, 2)[None]
 

time: 89.6 us -> 87.5 us (0.977)
  Pallas kernels: 88.8 us -> 86.7 us
    pallas_call x1, Pallas kernels: 2.5 us -> 1.42 us  [on_device(): pl.pallas_call(finish, out_shape=(jax.ShapeDtypeStruct(new.shape, BF16),...]
    pallas_call x1, Pallas kernels: 86.3 us -> 85.3 us  [on_device(): pl.pallas_call(functools.partial(kernel, {'chips': chips, 'n_z': n_z, 'n_...]
where the time goes in v5:
time: 87.5 us; the launch traced here: 87.3 us
  Pallas kernels  86.7 us (99%)
    pallas_call x1, Pallas kernels, on_device(): pl.pallas_call(functools.partial(kernel, {'chips': chips, 'n_z': n_z, 'n_...  85.3 us

profile of v5, /device:TPU:1, one launch (start us, length us, event | category | flops | bytes accessed | tf_op | source)
XLA Modules:
  0.0 87.3 jit_solution(10173110189113537361)
XLA Ops:
  0.6 85.3 %shard_map.95 = (bf16[384,2560]{1,0:T(8,128)(2,1)S(1)}, f32[96,8,128]{2,1,0:T(8,128)S(1)}) custom-call(bf16[1024,384]{1,0:T(8,128)(2,1)} %attn_hbm.1, bf16[128,2560]{1,0:T(8,128)(2,1)} %cot_hbm.1, bf16[384,2560]{1,0:T(8,128)(2,1)} %bitcast.13, s32[48,64]{1,0:T(8,128)} %bitcast.14, s32[1,64]{1,0:T(1,128)} %bitcast.16, s32[12,1,64]{2,1,0:T(1,128)} %bitcast.15, ...), custom_call_target="tpu_custom_call" | custom-call | tf_op jit(solution)/shard_map/pallas_call | solution.py:445
  85.9 1.4 %shard_map.96 = (bf16[384,2560]{1,0:T(8,128)(2,1)}, f32[96,8,128]{2,1,0:T(8,128)}) custom-call(bf16[384,2560]{1,0:T(8,128)(2,1)S(1)} %get-tuple-element.6.new_v, f32[96,8,128]{2,1,0:T(8,128)S(1)} %get-tuple-element.7.kept_v), custom_call_target="tpu_custom_call" | custom-call | tf_op jit(solution)/shard_map/pallas_call | solution.py:506
